TPU v7x, 32 devices: a whole 2x2x4 slice. The times are simulated.
32 devices in a mesh: task: 4 (over z), tile: 8 (over y, x, core).
Axes of the slice: x: 2, y: 2, z: 4, core: 2. Of those that a mesh axis runs over, the one named last changes fastest.
Arguments:
- adjusted: bfloat16 [8, 3584, 18944], P('task', 'tile'), may hold values from -6 to 6
- fisher: bfloat16 [8, 3584, 18944], P('task', 'tile'), may hold values from 0.0099487305 to 10
Outputs:
- merged: bfloat16 [3584, 18944], P(None, ('task', 'tile'))
All inputs are finite; a program needn't handle non-finite values.
Results may differ from a plain program's by a relative error of at most 0.001.
Values may be sent and summed in bfloat16 or wider, within the bound.
A program may use at most 256 MiB of HBM per device.

v0:
```python
import jax
import jax.numpy as jnp
from jax import lax
from jax.sharding import PartitionSpec as P


def body(adjusted, fisher):
    scaled = fisher.astype(jnp.float32)
    numerator = jnp.sum(scaled * adjusted.astype(jnp.float32), axis=0)
    denominator = jnp.sum(scaled, axis=0)
    summed_num, summed_den = (
        lax.psum_scatter(numerator, "task", scatter_dimension=1, tiled=True),
        lax.psum_scatter(denominator, "task", scatter_dimension=1, tiled=True),
    )
    owner_num, owner_den = (
        lax.all_to_all(summed_num, "tile", split_axis=1, concat_axis=0, tiled=True),
        lax.all_to_all(summed_den, "tile", split_axis=1, concat_axis=0, tiled=True),
    )
    merged = (owner_num / owner_den).astype(jnp.bfloat16)
    return merged


def solution(mesh):
    return jax.shard_map(
        body,
        mesh=mesh,
        in_specs=(P("task", "tile", None), P("task", "tile", None)),
        out_specs=P(None, ("task", "tile")),
        check_vma=False,
    )
```

profile of v0, /device:TPU:8, one launch (start us, length us, event | category | flops | bytes accessed | tf_op | source)
XLA Modules:
  0.0 1319.0 jit_solution(12959855648986320677)
XLA Ops:
  6.5 0.0 reduce-scatter.3.cloned.1.call-start
  6.5 39.8 %fusion = f32[448,18944]{1,0:T(8,128)} fusion(bf16[2,448,18944]{2,1,0:T(8,128)(2,1)} %param.3, bf16[2,448,18944]{2,1,0:T(8,128)(2,1)} %param.2), kind=kLoop, calls=%fused_computation.2 | loop fusion | flops 59408384 | bytes 101842944 | tf_op jit(solution)/shard_map/reduce_sum | solution.py:9
  46.3 0.0 reduce-scatter.3.cloned.1.call-update
  46.4 0.0 reduce-scatter.5.cloned.1.call-start
  46.4 32.2 %convert_reduce_fusion = f32[448,18944]{1,0:T(8,128)} fusion(bf16[2,448,18944]{2,1,0:T(8,128)(2,1)} %param.3), kind=kLoop, calls=%fused_computation | loop fusion | flops 25460736 | bytes 67895296 | tf_op jit(solution)/shard_map/reduce_sum | solution.py:10
  78.6 0.0 reduce-scatter.5.cloned.1.call-update
  78.6 525.7 %reduce-scatter.3.cloned.1.call-done = f32[448,4736]{1,0:T(8,128)} async-done(((f32[448,18944]{1,0:T(8,128)}), f32[448,4736]{1,0:T(8,128)}) %reduce-scatter.3.cloned.1.call-update) | async-done | bytes 8486928 | tf_op jit(solution)/shard_map/reduce_scatter | solution.py:12
  604.3 10.8 all_to_all.20
  615.2 9.7 copy.5
  624.9 5.0 all-to-all-start
  629.9 537.4 %reduce-scatter.5.cloned.1.call-done = f32[448,4736]{1,0:T(8,128)} async-done(((f32[448,18944]{1,0:T(8,128)}), f32[448,4736]{1,0:T(8,128)}) %reduce-scatter.5.cloned.1.call-update) | async-done | bytes 8486928 | tf_op jit(solution)/shard_map/reduce_scatter | solution.py:13
  1167.3 10.9 all_to_all.22
  1178.2 8.9 copy.6
  1187.1 0.0 all-to-all-done
  1187.1 108.4 %all_to_all.26 = f32[448,8,592]{2,0,1:T(8,128)} all-to-all(f32[448,8,592]{2,0,1:T(8,128)} %copy.6), channel_id=1, replica_groups=mesh['task'=4,'tile'=8] {'tile'}, dimensions={1} | all-to-all | bytes 16973824 | tf_op jit(solution)/shard_map/all_to_all | solution.py:17
  1295.5 9.6 divide_convert_fusion
  1305.1 7.1 copy.7
Async XLA Ops:
  6.5 597.8 %reduce-scatter.3.cloned.1.call-start = ((), (), s32[]{:S(2)}) async-start(), calls=%async_computation.4 | async-start | bytes 42434560 | tf_op jit(solution)/shard_map/reduce_scatter | solution.py:12
  46.4 1120.9 %reduce-scatter.5.cloned.1.call-start = ((), (), s32[]{:S(2)}) async-start(), calls=%async_computation.5 | async-start | bytes 42434560 | tf_op jit(solution)/shard_map/reduce_scatter | solution.py:13
  624.9 562.2 %all-to-all-start = ((f32[448,8,592]{2,0,1:T(8,128)}), f32[448,8,592]{2,0,1:T(8,128)}, u32[]{:S(2)}, u32[]{:S(2)}) async-start(f32[448,8,592]{2,0,1:T(8,128)} %copy.5), calls=%async_computation.1 | async-start | bytes 18350080 | tf_op jit(solution)/shard_map/all_to_all | solution.py:16
Sparse Core Ops, SparseCore 0:
  46.5 557.8 reduce-scatter.2
  606.7 560.5 reduce-scatter.4
where the time goes:
time: 1320 us
  waiting for transfers between devices  1060 us (80%)
  blocking collectives  108 us (8%)
  other arithmetic  81.6 us (6%)
  local copies, waits for them, and re-layouts  47.4 us (4%)
  between operations  13.4 us (1%)
    reduce_scatter x1, waiting for transfers between devices, body(): lax.psum_scatter(denominator, 'task', scatter_dimension=1, tiled=True)  537 us
    reduce_scatter x1, waiting for transfers between devices, body(): lax.psum_scatter(numerator, 'task', scatter_dimension=1, tiled=True)  526 us
    all_to_all x1, blocking collectives, body(): lax.all_to_all(summed_den, 'tile', split_axis=1, concat_axis=0, tiled=True)  108 us
    reduce_sum x1, other arithmetic, body(): numerator = jnp.sum(scaled * adjusted.astype(jnp.float32), axis=0)  39.8 us
    reduce_sum x1, other arithmetic, body(): denominator = jnp.sum(scaled, axis=0)  32.2 us
  transfers between devices with their start and end apart: 3, of which 2 were waited for; matrix products, arithmetic and copies ran while one was open for 4% of the time, Pallas kernels for 0%

commit v1 on v0

v1 whole, which is shorter than its diff:
```python
import functools
import math
import jax
import jax.numpy as jnp
from jax import lax
from jax.experimental import pallas as pl
from jax.experimental.pallas import tpu as pltpu
from jax.sharding import PartitionSpec as P

MESH = pl.DeviceIdType.MESH
LANES = 128
LOW, HIGH = 0.0099487305, 10.0
ODD, POWER = 15, 24
LIFT = 2.0**8.25


def over(count, step, carry, unroll=4):
    def trip(i, value):
        for u in range(unroll):
            value = step(i * unroll + u, value)
        return value

    carry = lax.fori_loop(0, count // unroll, trip, carry)
    for j in range(count // unroll * unroll, count):
        carry = step(j, carry)
    return carry


def kernel(n, rows, width, adj, fis, out, from_left, from_right, loc_a, loc_f, wire, got, num, den,
           loc_sem, send_sem, left_sem, right_sem, got_sem):
    me = lax.axis_index("task")
    chunks = out.shape[0] // rows
    blocks = width // LANES
    per_device = adj.shape[0] * math.sqrt(LOW * HIGH)
    f32 = jnp.float32

    def lanes(j, base=0):
        return pl.ds(pl.multiple_of(base + j * LANES, LANES), LANES)

    def loads(s, q, c, slot):
        where = (slice(None), pl.ds(pl.multiple_of(c * rows, rows), rows), pl.ds(pl.multiple_of(q * width, LANES), width))
        return (
            pltpu.make_async_copy(adj.at[where], loc_a.at[s, slot], loc_sem.at[s, slot, 0]),
            pltpu.make_async_copy(fis.at[where], loc_f.at[s, slot], loc_sem.at[s, slot, 1]),
        )

    def sending(s, q, c, slot):
        inbox, sem, to = ((from_left, left_sem, me + 1), (from_right, right_sem, me - 1))[s]
        return pltpu.make_async_remote_copy(
            src_ref=wire.at[s, slot], dst_ref=inbox.at[q, c], send_sem=send_sem.at[s, slot],
            recv_sem=sem.at[q * chunks + c], device_id={"task": to}, device_id_type=MESH)

    def local(s, slot):
        def step(j, carry):
            f, a = loc_f[s, slot, :, :, lanes(j)].astype(f32), loc_a[s, slot, :, :, lanes(j)].astype(f32)
            num[:, lanes(j)] = jnp.sum(f * a, axis=0)
            den[:, lanes(j)] = jnp.sum(f, axis=0)
            return carry

        over(blocks, step, 0)

    def arrive(side, q, c, held):
        sending(side, q, c, 0).wait_recv()
        inbox = (from_left, from_right)[side]
        copy = pltpu.make_async_copy(inbox.at[q, c], got.at[side], got_sem.at[side])
        copy.start()
        copy.wait()
        centre = per_device * held.astype(f32)
        unit = got[side, :, 2 * width:2 * width + LANES].astype(f32) * (1.0 / LIFT)

        def step(j, carry):
            y = got[side, :, lanes(j)].astype(f32)
            d = jnp.exp2(jnp.log2(got[side, :, lanes(j, width)].astype(f32)) * (1.0 / POWER)) * centre
            size = jnp.exp2(jnp.log2(jnp.maximum(jnp.abs(y), 2.0**-126)) * (1.0 / ODD)) * unit
            r = jnp.where(y < 0, -size, jnp.where(y > 0, size, 0.0))
            num[:, lanes(j)] += r * d
            den[:, lanes(j)] += d
            return carry

        over(blocks, step, 0)

    def encode(s, slot, held):
        def ratio(j, top):
            r = num[:, lanes(j)] / den[:, lanes(j)]
            num[:, lanes(j)] = r
            return jnp.maximum(top, jnp.abs(r))

        top = over(blocks, ratio, jnp.zeros((rows, LANES), f32))
        top = jnp.max(top, axis=1, keepdims=True)
        scale = jnp.broadcast_to(jnp.maximum(top * 1.01, 1e-35), (rows, LANES)).astype(jnp.bfloat16)
        wire[s, slot, :, 2 * width:2 * width + LANES] = scale
        factor = LIFT / scale.astype(f32)
        inverse = 1.0 / (per_device * held.astype(f32))

        def step(j, carry):
            x = num[:, lanes(j)] * factor
            x2 = x * x
            x4 = x2 * x2
            x8 = x4 * x4
            wire[s, slot, :, lanes(j)] = ((x * x2) * (x4 * x8)).astype(jnp.bfloat16)
            v = den[:, lanes(j)] * inverse
            v2 = v * v
            v4 = v2 * v2
            v8 = v4 * v4
            wire[s, slot, :, lanes(j, width)] = (v8 * v8 * v8).astype(jnp.bfloat16)
            return carry

        over(blocks, step, 0)

    def finish(c):
        def step(j, carry):
            merged = num[:, lanes(j)] / den[:, lanes(j)]
            out[pl.ds(pl.multiple_of(c * rows, rows), rows), lanes(j)] = merged.astype(jnp.bfloat16)
            return carry

        over(blocks, step, 0)

    has_left, has_right = me > 0, me < n - 1
    barrier = pltpu.get_barrier_semaphore()
    for there, to in ((has_left, me - 1), (has_right, me + 1)):
        @pl.when(there)
        def _():
            pl.semaphore_signal(barrier, inc=1, device_id={"task": to}, device_id_type=MESH)
    pl.semaphore_wait(barrier, has_left.astype(jnp.int32) + has_right.astype(jnp.int32))

    lasts = ((n - 1 - me) * chunks, me * chunks, chunks)
    quarter = (lambda i: n - 1 - i // chunks, lambda i: i // chunks, lambda i: me)

    def begin(s, i):
        for copy in loads(s, quarter[s](i), i % chunks, i % 2):
            copy.start()

    def work(s, i):
        q, c, slot = quarter[s](i), i % chunks, i % 2

        @pl.when(i + 1 < lasts[s])
        def _():
            begin(s, i + 1)

        for copy in loads(s, q, c, slot):
            copy.wait()
        local(s, slot)
        if s != 1:
            @pl.when(has_left)
            def _():
                arrive(0, q, c, me)
        if s != 0:
            @pl.when(has_right)
            def _():
                arrive(1, q, c, n - 1 - me)
        if s == 2:
            finish(c)
            return

        @pl.when(i >= 2)
        def _():
            sending(s, q, c, slot).wait_send()

        encode(s, slot, (me + 1, n - me)[s])
        sending(s, q, c, slot).start()

    for s in range(2):
        @pl.when(lasts[s] > 0)
        def _():
            begin(s, 0)
    begin(2, 0)
    late = (n - 2) * chunks

    def trip(t, carry):
        for s in range(2):
            @pl.when(t < lasts[s])
            def _():
                work(s, t)

        @pl.when(t >= late)
        def _():
            work(2, t - late)
        return carry

    lax.fori_loop(0, late + chunks, trip, 0)
    for s in range(2):
        @pl.when(lasts[s] > 0)
        def _():
            for slot in range(2):
                sending(s, 0, 0, slot).wait_send()


def body(n, adjusted, fisher):
    models, height, columns = adjusted.shape
    width = columns // n
    rows = next(r for r in (32, 16, 8, height) if height % r == 0)
    chunks = height // rows
    bf16 = jnp.bfloat16
    line = 2 * width + LANES
    merged, _, _ = pl.pallas_call(
        functools.partial(kernel, n, rows, width),
        out_shape=(
            jax.ShapeDtypeStruct((height, width), bf16),
            jax.ShapeDtypeStruct((n, chunks, rows, line), bf16),
            jax.ShapeDtypeStruct((n, chunks, rows, line), bf16),
        ),
        in_specs=[pl.BlockSpec(memory_space=pl.ANY)] * 2,
        out_specs=(pl.BlockSpec(memory_space=pltpu.VMEM), pl.BlockSpec(memory_space=pl.ANY), pl.BlockSpec(memory_space=pl.ANY)),
        scratch_shapes=[
            pltpu.VMEM((3, 2, models, rows, width), bf16),
            pltpu.VMEM((3, 2, models, rows, width), bf16),
            pltpu.VMEM((2, 2, rows, line), bf16),
            pltpu.VMEM((2, rows, line), bf16),
            pltpu.VMEM((rows, width), jnp.float32),
            pltpu.VMEM((rows, width), jnp.float32),
            pltpu.SemaphoreType.DMA((3, 2, 2)),
            pltpu.SemaphoreType.DMA((2, 2)),
            pltpu.SemaphoreType.DMA((n * chunks,)),
            pltpu.SemaphoreType.DMA((n * chunks,)),
            pltpu.SemaphoreType.DMA((2,)),
        ],
        compiler_params=pltpu.CompilerParams(collective_id=0, has_side_effects=True, vmem_limit_bytes=60 * 1024 * 1024),
    )(adjusted, fisher)
    return lax.all_to_all(merged, "tile", split_axis=1, concat_axis=0, tiled=True)


def solution(mesh):
    return jax.shard_map(
        functools.partial(body, mesh.shape["task"]),
        mesh=mesh,
        in_specs=(P("task", "tile", None), P("task", "tile", None)),
        out_specs=P(None, ("task", "tile")),
        check_vma=False,
    )
```

time: 1320 us -> 729 us (0.55)
  waiting for transfers between devices: 1060 us -> 0 us
  Pallas kernels: 0 us -> 650 us
  other arithmetic: 81.6 us -> 0 us
  blocking collectives: 108 us -> 56.9 us
  local copies, waits for them, and re-layouts: 47.4 us -> 19.4 us
  between operations: 13.4 us -> 0.01 us
    reduce_scatter x2 -> x0, waiting for transfers between devices: 1060 us -> none  [the longest x1 537 us: body(): lax.psum_scatter(denominator, 'task', scatter_dimension=1, tiled=True)]
    pallas_call x0 -> x1, Pallas kernels: none -> 650 us  [body(): pl.pallas_call(functools.partial(kernel, n, rows, width), out_shape=(jax....]
    reduce_sum x2 -> x0, other arithmetic: 72 us -> none  [the longest x1 39.8 us: body(): numerator = jnp.sum(scaled * adjusted.astype(jnp.float32), axis=0)]
    all_to_all x1, blocking collectives: 108 us -> 56.9 us  [body(): lax.all_to_all(merged, 'tile', split_axis=1, concat_axis=0, tiled=True)]
    all_to_all x4 -> x3, local copies, waits for them, and re-layouts: 40.3 us -> 19.4 us  [body(): lax.all_to_all(merged, 'tile', split_axis=1, concat_axis=0, tiled=True)]
  transfers between devices with their start and end apart: 3 -> 0, of which waited for: 2 -> 0; matrix products, arithmetic and copies ran while one was open for 4% -> 0% of each run, Pallas kernels for 0% -> 0%
where the time goes in v1:
time: 729 us; the launch traced here: 726 us
  Pallas kernels  650 us (89%)
  blocking collectives  56.9 us (8%)
  local copies, waits for them, and re-layouts  19.4 us (3%)
    pallas_call x1, Pallas kernels, body(): pl.pallas_call(functools.partial(kernel, n, rows, width), out_shape=(jax....  650 us
    all_to_all x1, blocking collectives, body(): lax.all_to_all(merged, 'tile', split_axis=1, concat_axis=0, tiled=True)  56.9 us
    all_to_all x3, local copies, waits for them, and re-layouts, body(): lax.all_to_all(merged, 'tile', split_axis=1, concat_axis=0, tiled=True)  19.4 us

profile of v1, /device:TPU:8, one launch (start us, length us, event | category | flops | bytes accessed | tf_op | source)
XLA Modules:
  0.0 726.4 jit_solution(7090876670345989861)
XLA Ops:
  0.0 650.2 %shard_map.28 = (bf16[448,4736]{1,0:T(8,128)(2,1)}, bf16[4,14,32,9600]{3,2,1,0:T(8,128)(2,1)}, bf16[4,14,32,9600]{3,2,1,0:T(8,128)(2,1)}) custom-call(bf16[2,448,18944]{2,1,0:T(8,128)(2,1)} %adj.1, bf16[2,448,18944]{2,1,0:T(8,128)(2,1)} %fis.1), custom_call_target="tpu_custom_call" | custom-call | tf_op jit(solution)/shard_map/pallas_call | solution.py:195
  650.2 9.4 %all_to_all.14 = bf16[448,8,592]{2,1,0:T(8,128)(2,1)} reshape(bf16[448,4736]{1,0:T(8,128)(2,1)} %get-tuple-element.6) | data formatting | bytes 8486912 | tf_op jit(solution)/shard_map/all_to_all | solution.py:219
  659.6 2.9 copy.4
  662.5 56.9 %all_to_all.19 = bf16[448,8,592]{2,0,1:T(8,128)(2,1)} all-to-all(bf16[448,8,592]{2,0,1:T(8,128)(2,1)S(1)} %copy.4), channel_id=1, replica_groups=mesh['task'=4,'tile'=8] {'tile'}, dimensions={1} | all-to-all | bytes 8486912 | tf_op jit(solution)/shard_map/all_to_all | solution.py:219
  719.4 7.1 copy.5
